TPU v7x, 32 devices: a whole 2x2x4 slice. The times are simulated.
32 devices in a mesh: groups: 2 (over y), tensor: 4 (over z), dp: 2 (over x), kv: 2 (over core).
Axes of the slice: x: 2, y: 2, z: 4, core: 2. Of those that a mesh axis runs over, the one named last changes fastest.
Arguments:
- residual: bfloat16 [64, 16384], P(('groups', 'dp'), ('tensor', 'kv')), parts along dimension 0, may hold values from -10 to 10
- query: bfloat16 [64, 8192], P(('groups', 'dp'), ('tensor', 'kv')), parts along dimension 0, may hold values from -60 to 60
- new_pair: bfloat16 [2, 64, 4, 128], P(None, ('groups', 'dp')), parts along dimension 1, may hold values from -8 to 8
- kv_cache: bfloat16 [2, 64, 2048, 4, 128], P(None, ('groups', 'dp'), ('tensor', 'kv')), parts along dimension 1, may hold values from -4.5 to 4.5
- lengths: int32 [64], P(('groups', 'dp')), parts along dimension 0, may hold values from 2 to 2048
- out_weight: bfloat16 [8192, 16384], P(('tensor', 'kv')), may hold values from -0.09375 to 0.09375
- norm_gain: bfloat16 [16384], replicated, may hold values from 0.25 to 1.75
Outputs:
- residual_out: bfloat16 [64, 16384], P(('groups', 'dp'), ('tensor', 'kv')), parts along dimension 0
- mlp_input: bfloat16 [64, 16384], P(('groups', 'dp')), parts along dimension 0
There are 2 independent parts, one for each index of `groups`. A program takes and returns all parts, laid end to end along the dimension named above; an argument that names none is the same for every part. Nothing has to cross between parts.
Inputs may be any that keep to these rules, and one draw needn't show every extreme that they name: Positions below lengths[b] hold sequence b's cache; the others are ignored.
All inputs are finite; a program needn't handle non-finite values.
Results may differ from a plain program's by a relative error of at most 0.007.
Values may be sent and summed in bfloat16 or wider, within the bound.
A program may use at most 128 MiB of HBM per device.

v0:
```python
import math
import jax
import jax.numpy as jnp
from jax import lax
from jax.sharding import PartitionSpec as P

D = 16384
QH = 64
KVH = 4
HD = 128
floor_value = -1e30
epsilon = 1e-05


def on_device(residual, query, new_pair, kv_cache, lengths, out_weight, norm_gain):
    seqs = residual.shape[0]
    width = residual.shape[1]
    per_dev = query.shape[1] // HD
    group = QH // KVH
    scaling = 1.0 / math.sqrt(HD)
    mine = lax.axis_index(("tensor", "kv"))
    queries = lax.all_gather(query, ("tensor", "kv"), axis=1, tiled=True)
    grouped = queries.reshape(seqs, KVH, group, HD)
    span = kv_cache.shape[2]
    places = mine * span + jnp.arange(span, dtype=jnp.int32)
    live = (places[None, :] < lengths[:, None])[:, None, None, :]
    scores = (
        jnp.einsum("bgjd,bpgd->bgjp", grouped, kv_cache[0], preferred_element_type=jnp.float32)
        * scaling
    )
    scores = jnp.where(live, scores, floor_value)
    highest = jnp.max(scores, axis=3)
    weights = jnp.where(live, jnp.exp(scores - highest[..., None]), 0.0)
    totals = jnp.sum(weights, axis=3)
    accum = jnp.einsum("bgjp,bpgd->bgjd", weights, kv_cache[1], preferred_element_type=jnp.float32)
    highest = highest.reshape(seqs, QH)
    totals = totals.reshape(seqs, QH)
    accum = accum.reshape(seqs, QH, HD)
    arrived = (
        lax.all_to_all(highest[None], ("tensor", "kv"), split_axis=2, concat_axis=0, tiled=True),
        lax.all_to_all(totals[None], ("tensor", "kv"), split_axis=2, concat_axis=0, tiled=True),
        lax.all_to_all(accum[None], ("tensor", "kv"), split_axis=2, concat_axis=0, tiled=True),
    )
    best = jnp.max(arrived[0], axis=0)
    factor = jnp.exp(arrived[0] - best[None])
    totals = jnp.sum(arrived[1] * factor, axis=0)
    accum = jnp.sum(arrived[2] * factor[..., None], axis=0)
    highest = best
    own_query = query.reshape(seqs, per_dev, HD).astype(jnp.float32)
    head_ids = mine * per_dev + jnp.arange(per_dev, dtype=jnp.int32)
    selector = (head_ids[:, None] // group == jnp.arange(KVH, dtype=jnp.int32)[None, :]).astype(
        jnp.float32
    )
    fresh_pair = jnp.einsum("hg,sbgd->sbhd", selector, new_pair.astype(jnp.float32))
    fresh = jnp.sum(own_query * fresh_pair[0], axis=2) * scaling
    best = jnp.maximum(highest, fresh)
    old_factor = jnp.exp(highest - best)
    new_factor = jnp.exp(fresh - best)
    totals = totals * old_factor + new_factor
    accum = accum * old_factor[..., None] + new_factor[..., None] * fresh_pair[1]
    attended = (accum / totals[..., None]).astype(jnp.bfloat16).reshape(seqs, per_dev * HD)
    partial_value = jnp.dot(attended, out_weight, preferred_element_type=jnp.float32)
    gain_wide = norm_gain.astype(jnp.float32)
    share = lax.psum_scatter(partial_value, ("tensor", "kv"), scatter_dimension=1, tiled=True)
    stream = (residual.astype(jnp.float32) + share).astype(jnp.bfloat16)
    widened = stream.astype(jnp.float32)
    squares = lax.psum(jnp.sum(widened * widened, axis=1), ("tensor", "kv"))
    gain_mine = lax.dynamic_slice_in_dim(gain_wide, mine * width, width, 0)
    piece = (widened * lax.rsqrt(squares / D + epsilon)[:, None] * gain_mine[None, :]).astype(
        jnp.bfloat16
    )
    normed = lax.all_gather(piece, ("tensor", "kv"), axis=1, tiled=True)
    return (stream, normed)


def solution(mesh):
    placed = (
        P(("groups", "dp"), ("tensor", "kv")),
        P(("groups", "dp"), ("tensor", "kv")),
        P(None, ("groups", "dp"), None, None),
        P(None, ("groups", "dp"), ("tensor", "kv"), None, None),
        P(("groups", "dp")),
        P(("tensor", "kv"), None),
        P(),
    )
    return jax.shard_map(
        on_device,
        mesh=mesh,
        in_specs=placed,
        out_specs=(P(("groups", "dp"), ("tensor", "kv")), P(("groups", "dp"), None)),
        check_vma=False,
    )
```

profile of v0, /device:TPU:0, one launch (start us, length us, event | category | flops | bytes accessed | tf_op | source)
XLA Modules:
  0.0 155.4 jit_solution(17761867516999163748)
XLA Ops:
  7.2 7.0 %fusion.25 = (bf16[1,16,256,4,128]{4,3,2,1,0:T(4,128)(2,1)}, bf16[1,16,256,4,128]{4,3,2,1,0:T(4,128)(2,1)S(1)}) fusion(bf16[2,16,256,4,128]{4,3,2,1,0:T(4,128)(2,1)} %param.10), kind=kLoop, calls=%fused_computation.48 | loop fusion | bytes 16777216 | tf_op jit(solution)/shard_map/slice | solution.py:35
  14.2 15.9 %all_gather.6 = bf16[16,8192]{1,0:T(8,128)(2,1)S(1)} all-gather(bf16[16,1024]{1,0:T(8,128)(2,1)S(1)} %copy-done.2), channel_id=1, replica_groups=mesh['groups'=2,'tensor'=4,'dp'=2,'kv'=2] {'tensor','kv'}, dimensions={1}, use_global_device_ids=true | all-gather | bytes 294912 | tf_op jit(solution)/shard_map/all_gather | solution.py:22
  30.3 1.3 fusion.26
  32.6 0.7 reduce.1
  33.3 0.7 reshape.118
  34.0 4.7 %all-to-all-start.2 = ((f32[8,1,128]{2,1,0:T(1,128)}), f32[8,1,128]{2,1,0:T(1,128)S(1)}, u32[]{:S(2)}, u32[]{:S(2)}) async-start(f32[8,1,128]{2,1,0:T(1,128)} %reshape.118), calls=%async_computation.2 | async-start | bytes 8192 | tf_op jit(solution)/shard_map/all_to_all | solution.py:41
  38.8 0.7 reduce.3
  39.5 0.7 reshape.116
  40.2 4.1 %all-to-all-done.2 = f32[8,1,128]{2,1,0:T(1,128)S(1)} async-done(((f32[8,1,128]{2,1,0:T(1,128)}), f32[8,1,128]{2,1,0:T(1,128)S(1)}, u32[]{:S(2)}, u32[]{:S(2)}) %all-to-all-start.2) | async-done | bytes 4128 | tf_op jit(solution)/shard_map/all_to_all | solution.py:41
  44.2 3.3 %all-to-all-start.1 = ((f32[8,1,128]{2,1,0:T(1,128)}), f32[8,1,128]{2,1,0:T(1,128)S(1)}, u32[]{:S(2)}, u32[]{:S(2)}) async-start(f32[8,1,128]{2,1,0:T(1,128)} %reshape.116), calls=%async_computation.1 | async-start | bytes 8192 | tf_op jit(solution)/shard_map/all_to_all | solution.py:40
  47.5 2.9 %fusion = f32[16,4,16,128]{3,2,1,0:T(8,128)S(1)} fusion(bf16[1,16,256,4,128]{4,3,2,1,0:T(4,128)(2,1)} %get-tuple-element.9, f32[16,4,16,256]{3,2,1,0:T(8,128)S(1)} %get-tuple-element.12, f32[16,4,16]{2,1,0:T(4,128)S(1)} %get-tuple-element.11, pred[16,256]{1,0:T(8,128)(4,1)S(1)} %broadcast_compare_fusion), kind=kOutput, calls=%fused_computation.1 | convolution fusion | flops 67633152 | bytes 5775360 | tf_op jit(solution)/shard_map/bgjp,bpgd->bgjd/dot_general | solution.py:35
  50.4 1.1 copy.34
  51.5 1.5 all-to-all-done.1
  53.0 3.5 %all-to-all-start = ((f32[1,16,64,128]{3,1,0,2:T(8,128)}), f32[1,16,64,128]{3,1,0,2:T(8,128)S(1)}, u32[]{:S(2)}, u32[]{:S(2)}) async-start(f32[1,16,64,128]{3,1,0,2:T(8,128)} %copy.34), calls=%async_computation | async-start | bytes 1048576 | tf_op jit(solution)/shard_map/all_to_all | solution.py:42
  57.0 0.6 reduce.2
  57.8 0.6 reduce.4
  58.7 13.1 %all-to-all-done = f32[1,16,64,128]{3,1,0,2:T(8,128)S(1)} async-done(((f32[1,16,64,128]{3,1,0,2:T(8,128)}), f32[1,16,64,128]{3,1,0,2:T(8,128)S(1)}, u32[]{:S(2)}, u32[]{:S(2)}) %all-to-all-start) | async-done | bytes 524320 | tf_op jit(solution)/shard_map/all_to_all | solution.py:42
  72.2 13.9 %fusion.15 = f32[16,16384]{1,0:T(8,128)} fusion(bf16[1024,16384]{1,0:T(8,128)(2,1)} %param.12, f32[2,8,8,128]{3,2,1,0:T(8,128)S(1)} %bitcast.90, f32[2,8,8,128]{3,2,1,0:T(8,128)S(1)} %bitcast.88, f32[2,8,8,128]{3,2,1,0:T(8,128)S(1)} %bitcast.89, f32[16,8,128]{2,0,1:T(8,128)S(1)} %multiply_reduce_fusion, f32[16,8]{0,1:T(8,128)S(1)} %get-tuple-element.5), kind=kOutput, calls=%fused_computation.28 | convolution fusion | flops 536952832 | bytes 34865664 | tf_op jit(solution)/shard_map/dot_general | solution.py:62
  86.2 0.7 dynamic-slice_convert_fusion
  86.9 31.0 %reduce-scatter.2.cloned.1.call-done = f32[16,2048]{1,0:T(8,128)} async-done(((f32[16,16384]{1,0:T(8,128)}), f32[16,2048]{1,0:T(8,128)}) %reduce-scatter.2.cloned.1.call-update) | async-done | bytes 131088 | tf_op jit(solution)/shard_map/reduce_scatter | solution.py:64
  117.9 1.0 fusion.8
  118.9 13.8 %psum.7 = f32[16]{0:T(128)S(1)} all-reduce(f32[16]{0:T(128)S(1)} %get-tuple-element.2), channel_id=1, replica_groups=mesh['groups'=2,'tensor'=4,'dp'=2,'kv'=2] {'tensor','kv'}, use_global_device_ids=true, to_apply=%region_8.9 | all-reduce | flops 16 | bytes 128 | tf_op jit(solution)/shard_map/psum | solution.py:67
  132.9 14.9 %all_gather.7 = bf16[16,16384]{1,0:T(8,128)(2,1)S(1)} all-gather(bf16[16,2048]{1,0:T(8,128)(2,1)S(1)} %fusion.10), channel_id=1, replica_groups=mesh['groups'=2,'tensor'=4,'dp'=2,'kv'=2] {'tensor','kv'}, dimensions={1}, use_global_device_ids=true | all-gather | bytes 589824 | tf_op jit(solution)/shard_map/all_gather | solution.py:72
  147.8 0.8 copy.70
  (38 shorter events, 2.6 us)
Async XLA Ops:
  7.2 49.5 %copy-start = (bf16[2,16,4,128]{3,2,1,0:T(4,128)(2,1)S(1)}, bf16[2,16,4,128]{3,2,1,0:T(4,128)(2,1)}, u32[]{:S(2)}) copy-start(bf16[2,16,4,128]{3,2,1,0:T(4,128)(2,1)} %param.9) | copy-start | bytes 98308
  7.2 7.0 %copy-start.2 = (bf16[16,1024]{1,0:T(8,128)(2,1)S(1)}, bf16[16,1024]{1,0:T(8,128)(2,1)}, u32[]{:S(2)}) copy-start(bf16[16,1024]{1,0:T(8,128)(2,1)} %param.8) | copy-start | bytes 98308
  7.2 23.0 %copy-start.4 = (s32[16]{0:T(128)S(1)}, s32[16]{0:T(128)}, u32[]{:S(2)}) copy-start(s32[16]{0:T(128)} %param.11) | copy-start | bytes 196
  34.0 10.2 %all-to-all-start.2 = ((f32[8,1,128]{2,1,0:T(1,128)}), f32[8,1,128]{2,1,0:T(1,128)S(1)}, u32[]{:S(2)}, u32[]{:S(2)}) async-start(f32[8,1,128]{2,1,0:T(1,128)} %reshape.118), calls=%async_computation.2 | async-start | bytes 8192 | tf_op jit(solution)/shard_map/all_to_all | solution.py:41
  44.2 8.8 %all-to-all-start.1 = ((f32[8,1,128]{2,1,0:T(1,128)}), f32[8,1,128]{2,1,0:T(1,128)S(1)}, u32[]{:S(2)}, u32[]{:S(2)}) async-start(f32[8,1,128]{2,1,0:T(1,128)} %reshape.116), calls=%async_computation.1 | async-start | bytes 8192 | tf_op jit(solution)/shard_map/all_to_all | solution.py:40
  53.0 18.9 %all-to-all-start = ((f32[1,16,64,128]{3,1,0,2:T(8,128)}), f32[1,16,64,128]{3,1,0,2:T(8,128)S(1)}, u32[]{:S(2)}, u32[]{:S(2)}) async-start(f32[1,16,64,128]{3,1,0,2:T(8,128)} %copy.34), calls=%async_computation | async-start | bytes 1048576 | tf_op jit(solution)/shard_map/all_to_all | solution.py:42
  56.5 61.3 %reduce-scatter.2.cloned.1.call-start = ((), (), s32[]{:S(2)}) async-start(), calls=%async_computation.4 | async-start | bytes 1179648 | tf_op jit(solution)/shard_map/reduce_scatter | solution.py:64
  72.2 45.7 %copy-start.3 = (bf16[16,2048]{1,0:T(8,128)(2,1)S(1)}, bf16[16,2048]{1,0:T(8,128)(2,1)}, u32[]{:S(2)}) copy-start(bf16[16,2048]{1,0:T(8,128)(2,1)} %param.7) | copy-start | bytes 196612
  118.9 29.7 %copy-start.1 = (bf16[16,2048]{1,0:T(8,128)(2,1)}, bf16[16,2048]{1,0:T(8,128)(2,1)S(1)}, u32[]{:S(2)}) copy-start(bf16[16,2048]{1,0:T(8,128)(2,1)S(1)} %get-tuple-element.15) | copy-start | bytes 196612
Sparse Core Ops, SparseCore 0:
  86.3 31.5 reduce-scatter.1
where the time goes:
time: 156 us; the launch traced here: 155 us
  waiting for transfers between devices  49.7 us (32%)
  blocking collectives  44.7 us (29%)
  matrix products  18.3 us (12%)
  between operations  14.2 us (9%)
  local copies, waits for them, and re-layouts  11.7 us (8%)
  starting transfers between devices  11.5 us (7%)
  other arithmetic  5.32 us (3%)
    reduce_scatter x1, waiting for transfers between devices, on_device(): lax.psum_scatter(partial_value, ('tensor', 'kv'), scatter_dimension=1, ti...  31 us
    all_gather x1, blocking collectives, on_device(): queries = lax.all_gather(query, ('tensor', 'kv'), axis=1, tiled=True)  15.9 us
    all_gather x1, blocking collectives, on_device(): normed = lax.all_gather(piece, ('tensor', 'kv'), axis=1, tiled=True)  14.9 us
    dot_general x1, matrix products, on_device(): jnp.dot(attended, out_weight, preferred_element_type=jnp.float32)  13.9 us
    psum x1, blocking collectives, on_device(): squares = lax.psum(jnp.sum(widened * widened, axis=1), ('tensor', 'kv'))  13.8 us
    all_to_all x1, waiting for transfers between devices, on_device(): lax.all_to_all(accum[None], ('tensor', 'kv'), split_axis=2, concat_axis=0...  13.1 us
    slice x1, local copies, waits for them, and re-layouts, on_device(): kv_cache[1]  7.01 us
    all_to_all x1, starting transfers between devices, on_device(): lax.all_to_all(totals[None], ('tensor', 'kv'), split_axis=2, concat_axis=...  4.68 us
  transfers between devices with their start and end apart: 4, of which 4 were waited for; matrix products, arithmetic and copies ran while one was open for 5% of the time, Pallas kernels for 0%

commit v1 on v0

--- a/solution.py
+++ b/solution.py
@@ -19,7 +19,7 @@
     group = QH // KVH
     scaling = 1.0 / math.sqrt(HD)
     mine = lax.axis_index(("tensor", "kv"))
-    queries = lax.all_gather(query, ("tensor", "kv"), axis=1, tiled=True)
+    queries = jnp.concatenate(lax.all_gather(query, ("tensor", "kv")), axis=1)
     grouped = queries.reshape(seqs, KVH, group, HD)
     span = kv_cache.shape[2]
     places = mine * span + jnp.arange(span, dtype=jnp.int32)

time: 156 us -> 159 us (1.019)
  matrix products: 18.3 us -> 20.5 us
    dot_general x1, matrix products: 1.3 us -> 3.48 us  [on_device(): jnp.einsum('bgjd,bpgd->bgjp', grouped, kv_cache[0], preferred_element_typ...]
where the time goes in v1:
time: 159 us
  waiting for transfers between devices  49.7 us (31%)
  blocking collectives  44.7 us (28%)
  matrix products  20.5 us (13%)
  between operations  14.2 us (9%)
  local copies, waits for them, and re-layouts  13 us (8%)
  starting transfers between devices  11.5 us (7%)
  other arithmetic  5.31 us (3%)
    reduce_scatter x1, waiting for transfers between devices, on_device(): lax.psum_scatter(partial_value, ('tensor', 'kv'), scatter_dimension=1, ti...  31 us
    all_gather x1, blocking collectives, on_device(): queries = jnp.concatenate(lax.all_gather(query, ('tensor', 'kv')), axis=1)  15.9 us
    all_gather x1, blocking collectives, on_device(): normed = lax.all_gather(piece, ('tensor', 'kv'), axis=1, tiled=True)  14.9 us
    dot_general x1, matrix products, on_device(): jnp.dot(attended, out_weight, preferred_element_type=jnp.float32)  13.9 us
    psum x1, blocking collectives, on_device(): squares = lax.psum(jnp.sum(widened * widened, axis=1), ('tensor', 'kv'))  13.8 us
    all_to_all x1, waiting for transfers between devices, on_device(): lax.all_to_all(accum[None], ('tensor', 'kv'), split_axis=2, concat_axis=0...  13.1 us
    slice x1, local copies, waits for them, and re-layouts, on_device(): kv_cache[1]  8.09 us
    all_to_all x1, starting transfers between devices, on_device(): lax.all_to_all(totals[None], ('tensor', 'kv'), split_axis=2, concat_axis=...  4.68 us
  transfers between devices with their start and end apart: 4, of which 4 were waited for; matrix products, arithmetic and copies ran while one was open for 5% of the time, Pallas kernels for 0%

profile of v1, /device:TPU:0, one launch (start us, length us, event | category | flops | bytes accessed | tf_op | source)
XLA Modules:
  0.0 158.9 jit_solution(16165509183633040035)
XLA Ops:
  7.2 8.1 %fusion.25 = (bf16[1,16,256,4,128]{4,3,2,1,0:T(4,128)(2,1)}, bf16[1,16,256,4,128]{4,3,2,1,0:T(4,128)(2,1)}) fusion(bf16[2,16,256,4,128]{4,3,2,1,0:T(4,128)(2,1)} %param.10), kind=kLoop, calls=%fused_computation.49 | loop fusion | bytes 16777216 | tf_op jit(solution)/shard_map/slice | solution.py:35
  15.3 15.9 %all-gather = bf16[128,1024]{1,0:T(8,128)(2,1)S(1)} all-gather(bf16[16,1024]{1,0:T(8,128)(2,1)S(1)} %copy-done.2), channel_id=2, replica_groups=mesh['groups'=2,'tensor'=4,'dp'=2,'kv'=2] {'tensor','kv'}, dimensions={0}, use_global_device_ids=true | all-gather | bytes 294912 | tf_op jit(solution)/shard_map/all_gather | solution.py:22
  31.6 3.5 %fusion.26 = (f32[16,4,16]{2,1,0:T(4,128)S(1)}, f32[16,4,16,256]{3,2,1,0:T(8,128)S(1)}) fusion(bf16[16,4,16,128]{3,2,1,0:T(8,128)(2,1)S(1)} %reshape_reshape.3, bf16[1,16,256,4,128]{4,3,2,1,0:T(4,128)(2,1)} %get-tuple-element.10, pred[16,256]{1,0:T(8,128)(4,1)S(1)} %broadcast_compare_fusion), kind=kOutput, calls=%fused_computation.50 | convolution fusion | flops 67894272 | bytes 5513216 | tf_op jit(solution)/shard_map/bgjd,bpgd->bgjp/dot_general | solution.py:28
  36.1 0.7 reduce.1
  36.8 0.7 reshape.119
  37.5 4.7 %all-to-all-start.2 = ((f32[8,1,128]{2,1,0:T(1,128)}), f32[8,1,128]{2,1,0:T(1,128)S(1)}, u32[]{:S(2)}, u32[]{:S(2)}) async-start(f32[8,1,128]{2,1,0:T(1,128)} %reshape.119), calls=%async_computation.2 | async-start | bytes 8192 | tf_op jit(solution)/shard_map/all_to_all | solution.py:41
  42.3 0.7 reduce.3
  43.0 0.7 reshape.117
  43.6 4.1 %all-to-all-done.2 = f32[8,1,128]{2,1,0:T(1,128)S(1)} async-done(((f32[8,1,128]{2,1,0:T(1,128)}), f32[8,1,128]{2,1,0:T(1,128)S(1)}, u32[]{:S(2)}, u32[]{:S(2)}) %all-to-all-start.2) | async-done | bytes 4128 | tf_op jit(solution)/shard_map/all_to_all | solution.py:41
  47.7 3.3 %all-to-all-start.1 = ((f32[8,1,128]{2,1,0:T(1,128)}), f32[8,1,128]{2,1,0:T(1,128)S(1)}, u32[]{:S(2)}, u32[]{:S(2)}) async-start(f32[8,1,128]{2,1,0:T(1,128)} %reshape.117), calls=%async_computation.1 | async-start | bytes 8192 | tf_op jit(solution)/shard_map/all_to_all | solution.py:40
  51.0 2.9 %fusion = f32[16,4,16,128]{3,2,1,0:T(8,128)S(1)} fusion(bf16[1,16,256,4,128]{4,3,2,1,0:T(4,128)(2,1)} %get-tuple-element.9, f32[16,4,16,256]{3,2,1,0:T(8,128)S(1)} %get-tuple-element.12, f32[16,4,16]{2,1,0:T(4,128)S(1)} %get-tuple-element.11, pred[16,256]{1,0:T(8,128)(4,1)S(1)} %broadcast_compare_fusion), kind=kOutput, calls=%fused_computation.1 | convolution fusion | flops 67633152 | bytes 5775360 | tf_op jit(solution)/shard_map/bgjp,bpgd->bgjd/dot_general | solution.py:35
  53.9 1.1 copy.39
  55.0 1.5 all-to-all-done.1
  56.5 3.5 %all-to-all-start = ((f32[1,16,64,128]{3,1,0,2:T(8,128)}), f32[1,16,64,128]{3,1,0,2:T(8,128)S(1)}, u32[]{:S(2)}, u32[]{:S(2)}) async-start(f32[1,16,64,128]{3,1,0,2:T(8,128)} %copy.39), calls=%async_computation | async-start | bytes 1048576 | tf_op jit(solution)/shard_map/all_to_all | solution.py:42
  60.5 0.6 reduce.2
  61.2 0.6 reduce.4
  62.2 13.1 %all-to-all-done = f32[1,16,64,128]{3,1,0,2:T(8,128)S(1)} async-done(((f32[1,16,64,128]{3,1,0,2:T(8,128)}), f32[1,16,64,128]{3,1,0,2:T(8,128)S(1)}, u32[]{:S(2)}, u32[]{:S(2)}) %all-to-all-start) | async-done | bytes 524320 | tf_op jit(solution)/shard_map/all_to_all | solution.py:42
  75.7 13.9 %fusion.15 = f32[16,16384]{1,0:T(8,128)} fusion(bf16[1024,16384]{1,0:T(8,128)(2,1)} %param.12, f32[2,8,8,128]{3,2,1,0:T(8,128)S(1)} %bitcast.91, f32[2,8,8,128]{3,2,1,0:T(8,128)S(1)} %bitcast.89, f32[2,8,8,128]{3,2,1,0:T(8,128)S(1)} %bitcast.90, f32[16,8,128]{2,0,1:T(8,128)S(1)} %multiply_reduce_fusion, f32[16,8]{0,1:T(8,128)S(1)} %get-tuple-element.5), kind=kOutput, calls=%fused_computation.29 | convolution fusion | flops 536952832 | bytes 34865664 | tf_op jit(solution)/shard_map/dot_general | solution.py:62
  89.7 0.7 dynamic-slice_convert_fusion
  90.4 31.0 %reduce-scatter.2.cloned.1.call-done = f32[16,2048]{1,0:T(8,128)} async-done(((f32[16,16384]{1,0:T(8,128)}), f32[16,2048]{1,0:T(8,128)}) %reduce-scatter.2.cloned.1.call-update) | async-done | bytes 131088 | tf_op jit(solution)/shard_map/reduce_scatter | solution.py:64
  121.4 1.0 fusion.8
  122.4 13.8 %psum.7 = f32[16]{0:T(128)S(1)} all-reduce(f32[16]{0:T(128)S(1)} %get-tuple-element.2), channel_id=1, replica_groups=mesh['groups'=2,'tensor'=4,'dp'=2,'kv'=2] {'tensor','kv'}, use_global_device_ids=true, to_apply=%region_8.9 | all-reduce | flops 16 | bytes 128 | tf_op jit(solution)/shard_map/psum | solution.py:67
  136.3 14.9 %all_gather.11 = bf16[16,16384]{1,0:T(8,128)(2,1)S(1)} all-gather(bf16[16,2048]{1,0:T(8,128)(2,1)S(1)} %fusion.10), channel_id=1, replica_groups=mesh['groups'=2,'tensor'=4,'dp'=2,'kv'=2] {'tensor','kv'}, dimensions={1}, use_global_device_ids=true | all-gather | bytes 589824 | tf_op jit(solution)/shard_map/all_gather | solution.py:72
  151.3 0.8 copy.76
  (39 shorter events, 2.8 us)
Async XLA Ops:
  7.2 52.9 %copy-start = (bf16[2,16,4,128]{3,2,1,0:T(4,128)(2,1)S(1)}, bf16[2,16,4,128]{3,2,1,0:T(4,128)(2,1)}, u32[]{:S(2)}) copy-start(bf16[2,16,4,128]{3,2,1,0:T(4,128)(2,1)} %param.9) | copy-start | bytes 98308
  7.2 8.1 %copy-start.2 = (bf16[16,1024]{1,0:T(8,128)(2,1)S(1)}, bf16[16,1024]{1,0:T(8,128)(2,1)}, u32[]{:S(2)}) copy-start(bf16[16,1024]{1,0:T(8,128)(2,1)} %param.8) | copy-start | bytes 98308
  7.2 24.3 %copy-start.4 = (s32[16]{0:T(128)S(1)}, s32[16]{0:T(128)}, u32[]{:S(2)}) copy-start(s32[16]{0:T(128)} %param.11) | copy-start | bytes 196
  37.5 10.2 %all-to-all-start.2 = ((f32[8,1,128]{2,1,0:T(1,128)}), f32[8,1,128]{2,1,0:T(1,128)S(1)}, u32[]{:S(2)}, u32[]{:S(2)}) async-start(f32[8,1,128]{2,1,0:T(1,128)} %reshape.119), calls=%async_computation.2 | async-start | bytes 8192 | tf_op jit(solution)/shard_map/all_to_all | solution.py:41
  47.7 8.8 %all-to-all-start.1 = ((f32[8,1,128]{2,1,0:T(1,128)}), f32[8,1,128]{2,1,0:T(1,128)S(1)}, u32[]{:S(2)}, u32[]{:S(2)}) async-start(f32[8,1,128]{2,1,0:T(1,128)} %reshape.117), calls=%async_computation.1 | async-start | bytes 8192 | tf_op jit(solution)/shard_map/all_to_all | solution.py:40
  56.5 18.9 %all-to-all-start = ((f32[1,16,64,128]{3,1,0,2:T(8,128)}), f32[1,16,64,128]{3,1,0,2:T(8,128)S(1)}, u32[]{:S(2)}, u32[]{:S(2)}) async-start(f32[1,16,64,128]{3,1,0,2:T(8,128)} %copy.39), calls=%async_computation | async-start | bytes 1048576 | tf_op jit(solution)/shard_map/all_to_all | solution.py:42
  60.0 61.3 %reduce-scatter.2.cloned.1.call-start = ((), (), s32[]{:S(2)}) async-start(), calls=%async_computation.4 | async-start | bytes 1179648 | tf_op jit(solution)/shard_map/reduce_scatter | solution.py:64
  75.7 45.7 %copy-start.3 = (bf16[16,2048]{1,0:T(8,128)(2,1)S(1)}, bf16[16,2048]{1,0:T(8,128)(2,1)}, u32[]{:S(2)}) copy-start(bf16[16,2048]{1,0:T(8,128)(2,1)} %param.7) | copy-start | bytes 196612
  122.4 29.7 %copy-start.1 = (bf16[16,2048]{1,0:T(8,128)(2,1)}, bf16[16,2048]{1,0:T(8,128)(2,1)S(1)}, u32[]{:S(2)}) copy-start(bf16[16,2048]{1,0:T(8,128)(2,1)S(1)} %get-tuple-element.15) | copy-start | bytes 196612
Sparse Core Ops, SparseCore 0:
  89.8 31.5 reduce-scatter.1
